TPU v7x, 32 devices: a whole 2x2x4 slice. The times are simulated.
32 devices in a mesh: section: 4 (over y, x), dev: 8 (over z, core).
Axes of the slice: x: 2, y: 2, z: 4, core: 2. Of those that a mesh axis runs over, the one named last changes fastest.
Arguments:
- patches: bfloat16 [4, 12288, 1280], P('section', 'dev'), may hold values from -6 to 6
- win_count: int32 [4, 8], P('section'), may hold values from 1 to 24, 64 in all within a row
- dest_perm: int32 [4, 8], P('section'), may hold values from 0 to 7, each once within a row
- win_groups: int32 [4, 8, 24], P('section'), may hold values from 2 to 16
- norm_gain: float32 [1280], replicated, may hold values from 0.5 to 1.5
- qkv_weight: bfloat16 [1280, 3840], P('dev')
- qkv_bias: float32 [3840], replicated, may hold values from -1.5 to 1.5
- proj_weight: bfloat16 [1280, 1280], P('dev'), may hold values from -0.15625 to 0.15625
- proj_bias: float32 [1280], replicated, may hold values from -1.5 to 1.5
- merge_gain: float32 [1280], replicated, may hold values from 0.5 to 1.5
- owner: int32 [4, 1024, 1], P('section', 'dev'), may hold values from 0 to 3; in each aligned block of 128 rows (0 to 127, 128 to 255, ..., all dimensions but the last counted through in order) at most 64 rows name the same one
Outputs:
- dispatched: bfloat16 [4, 2048, 5120], P('section', 'dev')
Inputs may be any that keep to these rules, and one draw needn't show every extreme that they name: `win_count`: within each section's row the counts sum to 8 times the devices of dev, and the largest is 24. `dest_perm`: each section's row is a permutation. `win_groups`: entries of slots past a device's count are not read. Among the 128 rows of one device, at most 64 have the same owner, and some device of every draw reaches 64.
All inputs are finite; a program needn't handle non-finite values.
Results may differ from a plain program's by a relative error of at most 0.0051.
Values may be sent and summed in bfloat16 or wider, within the bound.
A program may use at most 128 MiB of HBM per device.

v0:
```python
import jax
import jax.numpy as jnp
from jax import lax
from jax.sharding import PartitionSpec as P

D = 1280
HEADS = 16
WIN = 64
DST_WIN = 8
SRC_WIN = 24


def normalize(values, gain):
    return values * lax.rsqrt(jnp.mean(values * values, axis=-1, keepdims=True) + 1e-06) * gain


def contract(inputs, shard):
    section_count = lax.axis_size("section")
    dev_count = lax.axis_size("dev")
    sub_rows = shard.shape[0] // section_count
    portion = lax.dynamic_slice_in_dim(shard, lax.axis_index("section") * sub_rows, sub_rows, 0)
    height = inputs.shape[0]
    ordered = (
        inputs.reshape(height, dev_count, section_count, sub_rows)
        .transpose(0, 2, 1, 3)
        .reshape(height, -1)
    )
    whole = lax.all_gather(portion, ("section", "dev"), axis=0, tiled=True)
    return jnp.dot(ordered, whole, preferred_element_type=jnp.float32)


def encode(windows, groups, norm_gain, qkv_weight, qkv_bias, proj_weight, proj_bias, merge_gain):
    count = windows.shape[0]
    values = windows.reshape(count * WIN, D).astype(jnp.float32)
    normed = normalize(values, norm_gain).astype(jnp.bfloat16)
    triple = (contract(normed, qkv_weight) + qkv_bias).astype(jnp.bfloat16)
    triple = triple.reshape(count, WIN, 3, HEADS, D // HEADS)
    scores = jnp.einsum(
        "bqhe,bkhe->bhqk", triple[:, :, 0], triple[:, :, 1], preferred_element_type=jnp.float32
    )
    scores = scores * (D // HEADS) ** (-0.5)
    living = jnp.arange(WIN, dtype=jnp.int32)[None, :] < 4 * groups[:, None]
    scores = jnp.where(living[:, None, None, :], scores, -1e30)
    highest = jnp.max(scores, axis=-1, keepdims=True)
    powers = jnp.exp(scores - highest)
    probs = (powers / jnp.sum(powers, axis=-1, keepdims=True)).astype(jnp.bfloat16)
    mixed = jnp.einsum(
        "bhqk,bkhe->bqhe", probs, triple[:, :, 2], preferred_element_type=jnp.float32
    )
    mixed = mixed.astype(jnp.bfloat16).reshape(count * WIN, D)
    encoded = values + contract(mixed, proj_weight) + proj_bias
    final = normalize(encoded, merge_gain) * living.reshape(count * WIN, 1).astype(jnp.float32)
    return final.reshape(count * WIN // 4, 4 * D).astype(jnp.bfloat16)


def pack(merged, owners, section_count, capacity):
    sections = jnp.arange(section_count, dtype=jnp.int32)
    hits = (owners[:, None] == sections[None, :]).astype(jnp.int32)
    ranks = jnp.sum((jnp.cumsum(hits, axis=0) - hits) * hits, axis=1)
    places = owners * capacity + ranks
    chosen = places[None, :] == jnp.arange(section_count * capacity, dtype=jnp.int32)[:, None]
    ladder = jnp.arange(merged.shape[0], dtype=jnp.int32)
    indices = jnp.sum(chosen.astype(jnp.int32) * ladder[None, :], axis=1)
    filled = jnp.any(chosen, axis=1)
    return jnp.where(filled[:, None], merged[indices], jnp.zeros((), merged.dtype))


def body(
    patches,
    win_count,
    dest_perm,
    win_groups,
    norm_gain,
    qkv_weight,
    qkv_bias,
    proj_weight,
    proj_bias,
    merge_gain,
    owner,
):
    dev_count = lax.axis_size("dev")
    section_count = lax.axis_size("section")
    position = lax.axis_index("dev")
    windows = patches.reshape(SRC_WIN, WIN, D)
    counts = win_count[0]
    ladder = jnp.arange(dev_count, dtype=jnp.int32)
    before = jnp.sum(jnp.where(ladder[None, :] < ladder[:, None], counts[None, :], 0), axis=1)
    inverse = jnp.sum(
        ladder[:, None] * (dest_perm[0][:, None] == ladder[None, :]).astype(jnp.int32), axis=0
    )
    pair_slots = (SRC_WIN + dev_count - 1) // dev_count
    my_count = counts[position]
    begin_at = before[position]
    residue = jnp.mod(inverse - begin_at, dev_count)
    picked = jnp.arange(pair_slots, dtype=jnp.int32)[None, :] * dev_count + residue[:, None]
    usable = picked < my_count
    outgoing = jnp.where(
        usable[:, :, None, None],
        windows[jnp.minimum(picked, SRC_WIN - 1)],
        jnp.zeros((), windows.dtype),
    )
    outgoing = outgoing.reshape(dev_count * pair_slots * WIN, D)
    arrived = lax.all_to_all(outgoing, "dev", split_axis=0, concat_axis=0, tiled=True).reshape(
        dev_count, pair_slots, WIN, D
    )
    wanted = jnp.arange(DST_WIN, dtype=jnp.int32) * dev_count + inverse[position]
    source = jnp.sum((before[None, :] <= wanted[:, None]).astype(jnp.int32), axis=1) - 1
    within = wanted - before[source]
    balanced = arrived[source, within // dev_count]
    groups = win_groups[0][source, within]
    merged = encode(
        balanced, groups, norm_gain, qkv_weight, qkv_bias, proj_weight, proj_bias, merge_gain
    )
    merged_rows = merged.shape[0]
    capacity = 2 * merged_rows // section_count
    packed = pack(merged, owner[0, :, 0], section_count, capacity)
    delivered = lax.all_to_all(packed, "section", split_axis=0, concat_axis=0, tiled=True)
    return delivered.reshape(1, section_count * capacity, 4 * D)


def solution(mesh):
    return jax.shard_map(
        body,
        mesh=mesh,
        in_specs=(
            P("section", "dev", None),
            P("section", None),
            P("section", None),
            P("section", None, None),
            P(),
            P("dev", None),
            P(),
            P("dev", None),
            P(),
            P(),
            P("section", "dev", None),
        ),
        out_specs=P("section", "dev", None),
        check_vma=False,
    )
```

profile of v0, /device:TPU:0, one launch (start us, length us, event | category | flops | bytes accessed | tf_op | source)
XLA Modules:
  0.0 272.6 jit_solution(13226182876215991193)
XLA Ops:
  6.5 1.3 copy-done
  7.8 0.7 constant_dynamic-slice_fusion.1
  8.6 1.2 constant_dynamic-slice_fusion.2
  9.8 0.8 select_reduce_fusion.2
  10.6 0.6 dynamic_slice.15
  11.2 0.7 select_reduce_fusion.3
  11.9 0.6 and_select_fusion.1
  12.5 0.7 add_compare_fusion
  13.6 4.9 %gather_fusion = bf16[24,64,1280]{2,1,0:T(8,128)(2,1)} fusion(bf16[24,64,1280]{2,1,0:T(8,128)(2,1)} %bitcast.83, s32[1024]{0:T(1024)S(1)} %pad_clamp_fusion.2), kind=kCustom, calls=%fused_computation | custom fusion | bytes 7864416 | tf_op jit(solution)/shard_map/gather | solution.py:99
  18.5 3.8 %bitcast_select_fusion = bf16[8,192,1280]{2,1,0:T(8,128)(2,1)} fusion(pred[8,192]{1,0:T(8,128)(4,1)S(1)} %broadcast_in_dim.55, bf16[8,192,1280]{2,1,0:T(8,128)(2,1)} %bitcast.77), kind=kLoop, calls=%fused_computation.10 | loop fusion | flops 1966080 | bytes 7865856 | tf_op jit(solution)/shard_map/jit(_where)/select_n | solution.py:97
  22.3 6.6 %all-to-all-start = ((bf16[8,192,1280]{2,1,0:T(8,128)(2,1)}), bf16[8,192,1280]{2,1,0:T(8,128)(2,1)}, u32[]{:S(2)}, u32[]{:S(2)}) async-start(bf16[8,192,1280]{2,1,0:T(8,128)(2,1)} %bitcast_select_fusion), calls=%async_computation | async-start | bytes 7864320 | tf_op jit(solution)/shard_map/all_to_all | solution.py:103
  28.9 1.5 constant_dynamic-slice_fusion
  30.5 0.6 dynamic_slice.17
  31.1 0.6 multiply_add_fusion
  31.7 0.2 convert_reduce_fusion
  31.9 0.6 gather_fusion.1
  32.6 0.1 mul.141
  32.7 0.7 fusion.20
  33.4 0.6 gather_fusion.3
  34.3 0.2 reduce_window_sum.11
  34.4 0.2 select_reduce_fusion.1
  34.6 0.1 fusion.10
  34.8 0.1 select_reduce_fusion
  35.0 123.2 %all-to-all-done = bf16[8,192,1280]{2,1,0:T(8,128)(2,1)} async-done(((bf16[8,192,1280]{2,1,0:T(8,128)(2,1)}), bf16[8,192,1280]{2,1,0:T(8,128)(2,1)}, u32[]{:S(2)}, u32[]{:S(2)}) %all-to-all-start) | async-done | bytes 3932192 | tf_op jit(solution)/shard_map/all_to_all | solution.py:103
  158.2 2.7 %gather_fusion.2 = bf16[8,64,1280]{2,1,0:T(8,128)(2,1)S(1)} fusion(bf16[8,3,64,1280]{3,2,1,0:T(8,128)(2,1)} %bitcast.7, s32[8]{0:T(128)S(1)} %get-tuple-element.9), kind=kCustom, calls=%fused_computation.2 | custom fusion | bytes 2621504 | tf_op jit(solution)/shard_map/gather | solution.py:109
  161.0 3.7 %copy.32 = f32[8,64,1280]{1,0,2:T(8,128)} copy(bf16[8,64,1280]{2,1,0:T(8,128)(2,1)S(1)} %gather_fusion.2) | data formatting | bytes 3932160 | tf_op jit(solution)/shard_map/convert_element_type | solution.py:34
  164.6 1.7 convert_element_type.72
  166.4 5.0 %reshape.368 = f32[512,8,4,40]{0,3,2,1:T(8,128)} reshape(f32[8,64,1280]{1,0,2:T(8,128)} %copy.32) | data formatting | bytes 5242880 | tf_op jit(solution)/shard_map/convert_element_type | solution.py:34
  171.4 0.3 multiply_reduce_fusion.1
  171.8 2.1 fusion.9
  173.9 0.1 copy.33
  174.1 10.7 %add_convert_fusion = bf16[512,3840]{1,0:T(8,128)(2,1)} fusion(bf16[512,1280]{0,1:T(8,128)(2,1)S(1)} %bitcast.84, bf16[1280,3840]{1,0:T(8,128)(2,1)} %all-gather.3.cloned.1.call-done, f32[3840]{0:T(1024)S(1)} %copy-done.7), kind=kOutput, calls=%fused_computation.6 | convolution fusion | flops 5037096960 | bytes 15088640 | tf_op jit(solution)/shard_map/dot_general | solution.py:29
  184.8 12.9 %reshape.364 = bf16[8,64,3,16,80]{4,3,2,1,0:T(8,128)(2,1)} reshape(bf16[512,3840]{1,0:T(8,128)(2,1)} %add_convert_fusion) | data formatting | bytes 7864320 | tf_op jit(solution)/shard_map/reshape | solution.py:37
  197.7 4.5 %fusion.25 = (bf16[8,64,1,16,80]{4,3,2,1,0:T(8,128)(2,1)S(1)}, bf16[8,64,1,16,80]{4,3,2,1,0:T(8,128)(2,1)S(1)}, bf16[8,64,1,16,80]{4,3,2,1,0:T(8,128)(2,1)S(1)}) fusion(bf16[8,64,3,16,80]{4,3,2,1,0:T(8,128)(2,1)} %reshape.364), kind=kLoop, calls=%fused_computation.82 | loop fusion | bytes 7864320 | tf_op jit(solution)/shard_map/slice | solution.py:48
  202.2 1.2 fusion.4
  203.5 2.3 fusion.26
  205.8 1.2 convert_bitcast_fusion
  207.0 2.8 %copy.38 = bf16[8,64,16,80]{1,0,3,2:T(8,128)(2,1)} copy(bf16[8,64,16,80]{3,1,2,0:T(8,128)(2,1)S(1)} %convert_bitcast_fusion) | data formatting | bytes 2621440 | tf_op jit(solution)/shard_map/convert_element_type | solution.py:50
  209.8 3.8 %reshape_reshape.3 = bf16[512,8,4,40]{0,3,2,1:T(8,128)(2,1)S(1)} reshape(bf16[8,64,16,80]{1,0,3,2:T(8,128)(2,1)} %copy.38) | data formatting | bytes 2621440 | tf_op jit(solution)/shard_map/reshape;reshape | solution.py:24
  213.6 1.2 copy.39
  214.8 5.3 %multiply_reduce_fusion = (f32[512]{0:T(512)S(1)}, f32[512,1280]{1,0:T(8,128)S(1)}) fusion(f32[1280]{0:T(1024)S(1)} %copy-done.3, f32[512,1280]{1,0:T(8,128)} %bitcast.80, bf16[512,1280]{0,1:T(8,128)(2,1)} %bitcast.82, bf16[1280,1280]{1,0:T(8,128)(2,1)} %all-gather.5.cloned.1.call-done), kind=kOutput, calls=%fused_computation.15 | convolution fusion | flops 1680342528 | bytes 9837568 | tf_op jit(solution)/shard_map/dot_general | solution.py:29
  220.2 1.4 multiply_convert_fusion
  221.6 2.5 convert_element_type.71
  224.1 3.6 %gather_fusion.4 = bf16[256,5120]{1,0:T(8,128)(2,1)} fusion(bf16[128,5120]{1,0:T(8,128)(2,1)S(1)} %convert_element_type.71, s32[1024]{0:T(1024)S(1)} %pad_clamp_fusion), kind=kCustom, calls=%fused_computation.4 | custom fusion | bytes 5243904 | tf_op jit(solution)/shard_map/gather | solution.py:65
  227.7 2.0 broadcast_select_fusion
  229.7 34.0 %all_to_all.12 = bf16[4,64,5120]{2,1,0:T(8,128)(2,1)S(1)} all-to-all(bf16[4,64,5120]{2,1,0:T(8,128)(2,1)S(1)} %broadcast_select_fusion), channel_id=1, replica_groups=mesh['section'=4,'dev'=8] {'section'}, dimensions={0} | all-to-all | bytes 5242880 | tf_op jit(solution)/shard_map/all_to_all | solution.py:117
  263.6 1.5 copy.53
  265.1 0.7 copy-done.1
  (39 shorter events, 0.9 us)
Async XLA Ops:
  6.5 1.3 copy-start
  6.5 167.5 %all-gather.3.cloned.1.call-start = ((), (), s32[]{:S(2)}) async-start(), calls=%async_computation.2 | async-start | bytes 10137600 | tf_op jit(solution)/shard_map/all_gather | solution.py:28
  22.2 10.3 %copy-start.5 = (f32[1280]{0:T(1024)S(1)}, f32[1280]{0:T(1024)}, u32[]{:S(2)}) copy-start(f32[1280]{0:T(1024)} %param.15) | copy-start | bytes 15364
  22.3 11.1 %copy-start.2 = (s32[1,8,24]{2,1,0:T(8,128)S(1)}, s32[1,8,24]{2,1,0:T(8,128)}, u32[]{:S(2)}) copy-start(s32[1,8,24]{2,1,0:T(8,128)} %param.14) | copy-start | bytes 2308
  22.3 11.9 %copy-start.6 = (s32[1,128,1]{1,2,0:T(1,128)S(1)}, s32[1,128,1]{1,2,0:T(1,128)}, u32[]{:S(2)}) copy-start(s32[1,128,1]{1,2,0:T(1,128)} %param.21) | copy-start | bytes 1540
  22.3 136.0 %all-to-all-start = ((bf16[8,192,1280]{2,1,0:T(8,128)(2,1)}), bf16[8,192,1280]{2,1,0:T(8,128)(2,1)}, u32[]{:S(2)}, u32[]{:S(2)}) async-start(bf16[8,192,1280]{2,1,0:T(8,128)(2,1)} %bitcast_select_fusion), calls=%async_computation | async-start | bytes 7864320 | tf_op jit(solution)/shard_map/all_to_all | solution.py:103
  28.9 186.0 %all-gather.5.cloned.1.call-start = ((), (), s32[]{:S(2)}) async-start(), calls=%async_computation.3 | async-start | bytes 3379200 | tf_op jit(solution)/shard_map/all_gather | solution.py:28
  171.8 2.2 copy-start.7
  209.8 5.0 %copy-start.3 = (f32[1280]{0:T(1024)S(1)}, f32[1280]{0:T(1024)}, u32[]{:S(2)}) copy-start(f32[1280]{0:T(1024)} %param.19) | copy-start | bytes 15364
  214.8 5.4 %copy-start.4 = (f32[1280]{0:T(1024)S(1)}, f32[1280]{0:T(1024)}, u32[]{:S(2)}) copy-start(f32[1280]{0:T(1024)} %param.20) | copy-start | bytes 15364
  263.6 2.2 copy-start.1
Sparse Core Ops, SparseCore 0:
  10.4 142.4 all-gather.2
  155.7 57.7 all-gather.4
where the time goes:
time: 274 us; the launch traced here: 273 us
  waiting for transfers between devices  123 us (45%)
  local copies, waits for them, and re-layouts  57.8 us (21%)
  blocking collectives  34 us (12%)
  other arithmetic  18.8 us (7%)
  matrix products  18.5 us (7%)
  between operations  13.6 us (5%)
  starting transfers between devices  6.66 us (2%)
    all_to_all x1, waiting for transfers between devices, body(): lax.all_to_all(outgoing, 'dev', split_axis=0, concat_axis=0, tiled=True)  123 us
    all_to_all x1, blocking collectives, body(): lax.all_to_all(packed, 'section', split_axis=0, concat_axis=0, tiled=True)  34 us
    dot_general x2, matrix products, contract(): return jnp.dot(ordered, whole, preferred_element_type=jnp.float32)  16.1 us
    reshape x1, local copies, waits for them, and re-layouts, encode(): triple = triple.reshape(count, WIN, 3, HEADS, D // HEADS)  12.9 us
    convert_element_type x2, local copies, waits for them, and re-layouts, encode(): values = windows.reshape(count * WIN, D).astype(jnp.float32)  8.7 us
    all_to_all x1, starting transfers between devices, body(): lax.all_to_all(outgoing, 'dev', split_axis=0, concat_axis=0, tiled=True)  6.62 us
  transfers between devices with their start and end apart: 3, of which 1 were waited for; matrix products, arithmetic and copies ran while one was open for 28% of the time, Pallas kernels for 0%

commit v1 on v0

v1 whole, which is shorter than its diff:
```python
import functools

import jax
import jax.numpy as jnp
from jax import lax
from jax.experimental import pallas as pl
from jax.experimental.pallas import tpu as pltpu
from jax.sharding import PartitionSpec as P

D = 1280
HEADS = 16
HEAD_DIM = D // HEADS
WIN = 64
DST_WIN = 8
SRC_WIN = 24
PAIR = 2 * WIN
CHUNK = 768


def whole_weight(shard):
    section_count = lax.axis_size("section")
    dev_count = lax.axis_size("dev")
    sub_rows = shard.shape[0] // section_count
    portion = lax.dynamic_slice_in_dim(shard, lax.axis_index("section") * sub_rows, sub_rows, 0)
    gathered = lax.all_gather(portion, ("section", "dev"), axis=0, tiled=True)
    return (
        gathered.reshape(section_count, dev_count, sub_rows, shard.shape[1])
        .transpose(1, 0, 2, 3)
        .reshape(section_count * dev_count * sub_rows, shard.shape[1])
    )


def normalize(values, gain):
    return values * lax.rsqrt(jnp.mean(values * values, axis=-1, keepdims=True) + 1e-06) * gain


def encode_kernel(
    steps, x_ref, gain_ref, w_ref, wb_ref, pw_ref, pb_ref, mg_ref, row_ref, key_ref, pick_ref,
    out_ref, normed, qkv, mixed, enc, tall, merged,
):
    step = pl.program_id(0)
    rows = x_ref.shape[0]

    @pl.when(step == 0)
    def _():
        @pl.loop(0, rows // WIN)
        def _(i):
            at = pl.ds(pl.multiple_of(i * WIN, WIN), WIN)
            normed[at, :] = normalize(x_ref[at, :].astype(jnp.float32), gain_ref[...]).astype(jnp.bfloat16)

    cols = pl.ds(pl.multiple_of(step * CHUNK, CHUNK), CHUNK)
    qkv[:, cols] = (
        jnp.dot(normed[...], w_ref[...], preferred_element_type=jnp.float32) + wb_ref[...]
    ).astype(jnp.bfloat16)

    @pl.when(step == steps - 1)
    def _():
        same = (
            lax.broadcasted_iota(jnp.int32, (PAIR, PAIR), 0) // WIN
            == lax.broadcasted_iota(jnp.int32, (PAIR, PAIR), 1) // WIN
        )

        @pl.loop(0, rows // PAIR)
        def _(pair):
            at = pl.ds(pl.multiple_of(pair * PAIR, PAIR), PAIR)
            valid = same & (key_ref[pair] > 0.5)
            blocks = [None] * (D // 128)
            for h in range(HEADS):
                low, high = h * HEAD_DIM, (h + 1) * HEAD_DIM
                begin, end = low // 128 * 128, -(-high // 128) * 128
                lane = lax.broadcasted_iota(jnp.int32, (1, end - begin), 1) + begin
                inside = ((lane >= low) & (lane < high)).astype(jnp.bfloat16)
                q = qkv[at, begin:end] * inside
                k = qkv[at, D + begin:D + end]
                v = qkv[at, 2 * D + begin:2 * D + end] * inside
                scores = lax.dot_general(
                    q, k, (((1,), (1,)), ((), ())), preferred_element_type=jnp.float32
                ) * HEAD_DIM ** (-0.5)
                scores = jnp.where(valid, scores, -1e30)
                powers = jnp.exp(scores - jnp.max(scores, axis=-1, keepdims=True))
                probs = (powers / jnp.sum(powers, axis=-1, keepdims=True)).astype(jnp.bfloat16)
                o = jnp.dot(probs, v, preferred_element_type=jnp.float32)
                for b in range(begin // 128, end // 128):
                    piece = o[:, b * 128 - begin:(b + 1) * 128 - begin]
                    blocks[b] = piece if blocks[b] is None else blocks[b] + piece
            for b in range(D // 128):
                mixed[at, b * 128:(b + 1) * 128] = blocks[b].astype(jnp.bfloat16)

        enc[...] = jnp.dot(mixed[...], pw_ref[...], preferred_element_type=jnp.float32)

        @pl.loop(0, rows // WIN)
        def _(i):
            at = pl.ds(pl.multiple_of(i * WIN, WIN), WIN)
            encoded = x_ref[at, :].astype(jnp.float32) + enc[at, :] + pb_ref[...]
            final = normalize(encoded, mg_ref[...]) * row_ref[at, :]
            for b in range(D // 128):
                tall[b, at, :] = final[:, b * 128:(b + 1) * 128]

        count = rows // 4
        for j in range(4):
            for b in range(D // 128):
                merged[:, j * D + b * 128:j * D + (b + 1) * 128] = tall[
                    b, pl.ds(j, count, stride=4), :
                ].astype(jnp.bfloat16)

        @pl.loop(0, 4)
        def _(j):
            at = pl.ds(pl.multiple_of(j * D, D), D)
            out_ref[:, at] = jnp.dot(
                pick_ref[...], merged[:, at], preferred_element_type=jnp.float32
            ).astype(jnp.bfloat16)


def encode(x, row_live, key_live, pick, norm_gain, qkv_w, qkv_bias, proj_w, proj_bias, merge_gain):
    rows = x.shape[0]
    steps = 3 * D // CHUNK
    slots = pick.shape[0]

    def full(*shape):
        return pl.BlockSpec(shape, lambda i: (0,) * len(shape))

    return pl.pallas_call(
        functools.partial(encode_kernel, steps),
        grid=(steps,),
        in_specs=[
            full(rows, D),
            full(1, D),
            pl.BlockSpec((D, CHUNK), lambda i: (0, i)),
            pl.BlockSpec((1, CHUNK), lambda i: (0, i)),
            full(D, D),
            full(1, D),
            full(1, D),
            full(rows, 1),
            full(rows // PAIR, 1, PAIR),
            full(slots, rows // 4),
        ],
        out_specs=full(slots, 4 * D),
        out_shape=jax.ShapeDtypeStruct((slots, 4 * D), jnp.bfloat16),
        scratch_shapes=[
            pltpu.VMEM((rows, D), jnp.bfloat16),
            pltpu.VMEM((rows, 3 * D), jnp.bfloat16),
            pltpu.VMEM((rows, D), jnp.bfloat16),
            pltpu.VMEM((rows, D), jnp.float32),
            pltpu.VMEM((D // 128, rows, 128), jnp.float32),
            pltpu.VMEM((rows // 4, 4 * D), jnp.bfloat16),
        ],
        compiler_params=pltpu.CompilerParams(
            dimension_semantics=("arbitrary",), vmem_limit_bytes=56 * 1024 * 1024
        ),
        cost_estimate=pl.CostEstimate(
            flops=2 * rows * D * 4 * D, bytes_accessed=8 * D * D + 6 * rows * D, transcendentals=0
        ),
    )(
        x, norm_gain[None], qkv_w, qkv_bias[None], proj_w, proj_bias[None], merge_gain[None],
        row_live, key_live, pick,
    )


def picking(owners, section_count, capacity):
    sections = jnp.arange(section_count, dtype=jnp.int32)
    hits = (owners[:, None] == sections[None, :]).astype(jnp.int32)
    ranks = jnp.sum((jnp.cumsum(hits, axis=0) - hits) * hits, axis=1)
    places = owners * capacity + ranks
    return places[None, :] == jnp.arange(section_count * capacity, dtype=jnp.int32)[:, None]


def body(
    patches,
    win_count,
    dest_perm,
    win_groups,
    norm_gain,
    qkv_weight,
    qkv_bias,
    proj_weight,
    proj_bias,
    merge_gain,
    owner,
):
    dev_count = lax.axis_size("dev")
    section_count = lax.axis_size("section")
    position = lax.axis_index("dev")
    windows = patches.reshape(SRC_WIN, WIN, D)
    counts = win_count[0]
    ladder = jnp.arange(dev_count, dtype=jnp.int32)
    before = jnp.sum(jnp.where(ladder[None, :] < ladder[:, None], counts[None, :], 0), axis=1)
    inverse = jnp.sum(
        ladder[:, None] * (dest_perm[0][:, None] == ladder[None, :]).astype(jnp.int32), axis=0
    )
    pair_slots = (SRC_WIN + dev_count - 1) // dev_count
    residue = jnp.mod(inverse - before[position], dev_count)
    picked = jnp.arange(pair_slots, dtype=jnp.int32)[None, :] * dev_count + residue[:, None]
    outgoing = windows[jnp.minimum(picked, SRC_WIN - 1)].reshape(dev_count * pair_slots * WIN, D)
    arrived = lax.all_to_all(outgoing, "dev", split_axis=0, concat_axis=0, tiled=True).reshape(
        dev_count * pair_slots, WIN, D
    )
    wanted = jnp.arange(DST_WIN, dtype=jnp.int32) * dev_count + inverse[position]
    source = jnp.sum((before[None, :] <= wanted[:, None]).astype(jnp.int32), axis=1) - 1
    within = wanted - before[source]
    balanced = arrived[source * pair_slots + within // dev_count].reshape(DST_WIN * WIN, D)
    groups = win_groups[0][source, within]
    living = (jnp.arange(WIN, dtype=jnp.int32)[None, :] < 4 * groups[:, None]).astype(jnp.float32)

    merged_rows = DST_WIN * WIN // 4
    capacity = 2 * merged_rows // section_count
    pick = picking(owner[0, :, 0], section_count, capacity).astype(jnp.bfloat16)
    packed = encode(
        balanced,
        living.reshape(DST_WIN * WIN, 1),
        living.reshape(DST_WIN * WIN // PAIR, 1, PAIR),
        pick,
        norm_gain,
        whole_weight(qkv_weight),
        qkv_bias,
        whole_weight(proj_weight),
        proj_bias,
        merge_gain,
    )
    delivered = lax.all_to_all(packed, "section", split_axis=0, concat_axis=0, tiled=True)
    return delivered.reshape(1, section_count * capacity, 4 * D)


def solution(mesh):
    return jax.shard_map(
        body,
        mesh=mesh,
        in_specs=(
            P("section", "dev", None),
            P("section", None),
            P("section", None),
            P("section", None, None),
            P(),
            P("dev", None),
            P(),
            P("dev", None),
            P(),
            P(),
            P("section", "dev", None),
        ),
        out_specs=P("section", "dev", None),
        check_vma=False,
    )
```

time: 274 us -> 279 us (1.018)
  waiting for transfers between devices: 123 us -> 157 us
  Pallas kernels: 0 us -> 29.2 us
  local copies, waits for them, and re-layouts: 57.8 us -> 31 us
  matrix products: 18.5 us -> 0 us
  other arithmetic: 18.8 us -> 5.46 us
    all_gather x2, waiting for transfers between devices: 0.02 us -> 141 us  [whole_weight(): gathered = lax.all_gather(portion, ('section', 'dev'), axis=0, tiled=True)]
    all_to_all x1, waiting for transfers between devices: 123 us -> 16.5 us  [body(): lax.all_to_all(outgoing, 'dev', split_axis=0, concat_axis=0, tiled=True)]
    pallas_call x0 -> x1, Pallas kernels: none -> 29.2 us  [encode(): pl.pallas_call(functools.partial(encode_kernel, steps), grid=(steps,), in...]
    dot_general x4 -> x0, matrix products: 18.5 us -> none  [the longest x2 16.1 us: contract(): return jnp.dot(ordered, whole, preferred_element_type=jnp.float32)]
    convert_element_type x5 -> x1, local copies, waits for them, and re-layouts: 14.1 us -> 0.89 us  [body(): (jnp.arange(WIN, dtype=jnp.int32)[None, :] < 4 * groups[:, None]).astype(...]
    select_n x5 -> x2, other arithmetic: 6.34 us -> 0.64 us  [the longest x1 0.64 us: body(): residue = jnp.mod(inverse - before[position], dev_count)]
    slice x1 -> x0, local copies, waits for them, and re-layouts: 4.54 us -> none  [encode(): triple[:, :, 2]]
    another operation x1 -> x0, local copies, waits for them, and re-layouts: 3.82 us -> none  [contract(): inputs.reshape(height, dev_count, section_count, sub_rows)]
  transfers between devices with their start and end apart: 3 -> 3, of which waited for: 1 -> 3; matrix products, arithmetic and copies ran while one was open for 28% -> 9% of each run, Pallas kernels for 0% -> 0%
where the time goes in v1:
time: 279 us; the launch traced here: 278 us
  waiting for transfers between devices  157 us (56%)
  blocking collectives  35.3 us (13%)
  local copies, waits for them, and re-layouts  31 us (11%)
  Pallas kernels  29.2 us (10%)
  between operations  13.5 us (5%)
  starting transfers between devices  6.54 us (2%)
  other arithmetic  5.46 us (2%)
    all_gather x2, waiting for transfers between devices, whole_weight(): gathered = lax.all_gather(portion, ('section', 'dev'), axis=0, tiled=True)  141 us
    all_to_all x1, blocking collectives, body(): lax.all_to_all(packed, 'section', split_axis=0, concat_axis=0, tiled=True)  35.3 us
    pallas_call x1, Pallas kernels, encode(): pl.pallas_call(functools.partial(encode_kernel, steps), grid=(steps,), in...  29.2 us
    all_to_all x1, waiting for transfers between devices, body(): lax.all_to_all(outgoing, 'dev', split_axis=0, concat_axis=0, tiled=True)  16.5 us
    reshape x2, local copies, waits for them, and re-layouts, whole_weight(): gathered.reshape(section_count, dev_count, sub_rows, shard.shape[1])  12.2 us
    all_to_all x1, starting transfers between devices, body(): lax.all_to_all(outgoing, 'dev', split_axis=0, concat_axis=0, tiled=True)  6.5 us
  transfers between devices with their start and end apart: 3, of which 3 were waited for; matrix products, arithmetic and copies ran while one was open for 9% of the time, Pallas kernels for 0%

profile of v1, /device:TPU:0, one launch (start us, length us, event | category | flops | bytes accessed | tf_op | source)
XLA Modules:
  0.0 278.3 jit_solution(11553629138223942168)
XLA Ops:
  6.5 0.0 copy-start
  6.5 1.6 constant_dynamic-slice_fusion
  8.2 0.0 all-gather.5.cloned.1.call-update
  8.2 0.0 all-gather.3.cloned.1.call-start
  8.2 0.0 copy-done
  8.3 0.7 constant_dynamic-slice_fusion.1
  9.0 0.0 all-gather.3.cloned.1.call-update
  9.0 0.8 select_reduce_fusion.1
  9.8 0.6 dynamic_slice.12
  10.4 0.7 select_reduce_fusion.2
  11.2 0.6 and_select_fusion.1
  11.8 0.1 compare_select_fusion
  11.9 0.1 reshape.320
  12.0 4.9 %gather_fusion = bf16[24,64,1280]{2,1,0:T(8,128)(2,1)} fusion(bf16[24,64,1280]{2,1,0:T(8,128)(2,1)} %bitcast.57, s32[1024]{0:T(1024)S(1)} %pad_clamp_fusion.2), kind=kCustom, calls=%fused_computation | custom fusion | bytes 7864416 | tf_op jit(solution)/shard_map/gather | solution.py:193
  16.9 0.0 copy-start.1
  16.9 0.0 copy-start.6
  16.9 6.5 %all-to-all-start = ((bf16[8,192,1280]{2,1,0:T(8,128)(2,1)}), bf16[8,192,1280]{2,1,0:T(8,128)(2,1)}, u32[]{:S(2)}, u32[]{:S(2)}) async-start(bf16[8,192,1280]{2,1,0:T(8,128)(2,1)} %bitcast.53), calls=%async_computation | async-start | bytes 7864320 | tf_op jit(solution)/shard_map/all_to_all | solution.py:194
  23.4 0.6 dynamic_slice.13
  24.1 0.6 multiply_add_fusion.1
  24.7 0.2 convert_reduce_fusion
  24.9 0.6 gather_fusion.1
  25.5 0.6 broadcast_in_dim.22.gain_ref
  26.1 0.6 broadcast_in_dim.23.wb_ref
  26.8 0.6 broadcast_in_dim.24.pb_ref
  27.4 0.0 copy-done.5
  27.4 0.6 broadcast_in_dim.25.mg_ref
  28.0 0.6 fusion.9
  28.6 0.6 gather_fusion.3
  29.3 0.1 mul.85
  29.3 0.1 fusion.2
  29.4 0.9 reshape.350.row_ref
  30.3 0.1 lt.109
  30.4 0.1 lt.110
  30.5 0.1 lt.107
  30.6 0.1 fusion.1
  30.7 0.2 reduce_window_sum.11
  30.8 0.2 select_reduce_fusion
  31.0 0.6 compare_convert_fusion.key_ref
  31.6 0.6 fusion.pick_ref
  32.3 78.0 %all-gather.5.cloned.1.call-done = bf16[1280,1280]{1,0:T(8,128)(2,1)} async-done(((bf16[40,1280]{1,0:T(8,128)(2,1)}), bf16[1280,1280]{1,0:T(8,128)(2,1)}) %all-gather.5.cloned.1.call-update) | async-done | bytes 3276816 | tf_op jit(solution)/shard_map/all_gather | solution.py:25
  110.3 3.9 %copy.18 = bf16[4,8,40,1280]{3,2,0,1:T(8,128)(2,1)} copy(bf16[4,8,40,1280]{3,2,1,0:T(8,128)(2,1)} %bitcast.58) | data formatting | bytes 6553600 | tf_op jit(solution)/shard_map/reshape | solution.py:27
  114.2 16.5 %all-to-all-done = bf16[8,192,1280]{2,1,0:T(8,128)(2,1)} async-done(((bf16[8,192,1280]{2,1,0:T(8,128)(2,1)}), bf16[8,192,1280]{2,1,0:T(8,128)(2,1)}, u32[]{:S(2)}, u32[]{:S(2)}) %all-to-all-start) | async-done | bytes 3932192 | tf_op jit(solution)/shard_map/all_to_all | solution.py:194
  130.7 3.8 %gather_fusion.2 = bf16[8,64,1280]{2,1,0:T(8,128)(2,1)} fusion(bf16[24,64,1280]{2,1,0:T(8,128)(2,1)} %bitcast.5, s32[1024]{0:T(1024)S(1)} %pad_clamp_fusion), kind=kCustom, calls=%fused_computation.2 | custom fusion | bytes 2621472 | tf_op jit(solution)/shard_map/gather | solution.py:200
  134.5 62.6 %all-gather.3.cloned.1.call-done = bf16[1280,3840]{1,0:T(8,128)(2,1)} async-done(((bf16[40,3840]{1,0:T(8,128)(2,1)}), bf16[1280,3840]{1,0:T(8,128)(2,1)}) %all-gather.3.cloned.1.call-update) | async-done | bytes 9830416 | tf_op jit(solution)/shard_map/all_gather | solution.py:25
  197.2 8.3 %copy.17 = bf16[4,8,40,3840]{3,2,0,1:T(8,128)(2,1)} copy(bf16[4,8,40,3840]{3,2,1,0:T(8,128)(2,1)} %bitcast.55) | data formatting | bytes 19660800 | tf_op jit(solution)/shard_map/reshape | solution.py:27
  205.5 29.2 %shard_map.109 = bf16[256,5120]{1,0:T(8,128)(2,1)} custom-call(bf16[512,1280]{1,0:T(8,128)(2,1)} %bitcast.61, f32[1,1280]{1,0:T(1,128)} %broadcast_in_dim.22.gain_ref, bf16[1280,3840]{1,0:T(8,128)(2,1)} %bitcast.56, f32[1,3840]{1,0:T(1,128)} %broadcast_in_dim.23.wb_ref, bf16[1280,1280]{1,0:T(8,128)(2,1)} %bitcast.59, f32[1,1280]{1,0:T(1,128)} %broadcast_in_dim.24.pb_ref, ...), custom_call_target="tpu_custom_call" | custom-call | flops 6710886400 | bytes 17039360 | tf_op jit(solution)/shard_map/pallas_call | solution.py:122
  234.7 35.3 %all_to_all.18 = bf16[4,64,5120]{2,1,0:T(8,128)(2,1)S(1)} all-to-all(bf16[4,64,5120]{2,1,0:T(8,128)(2,1)} %bitcast.60), channel_id=1, replica_groups=mesh['section'=4,'dev'=8] {'section'}, dimensions={0} | all-to-all | bytes 5242880 | tf_op jit(solution)/shard_map/all_to_all | solution.py:219
  270.0 1.5 copy.21
  (18 shorter events, 0.1 us)
Async XLA Ops:
  6.5 1.7 copy-start
  6.5 103.8 %all-gather.5.cloned.1.call-start = ((), (), s32[]{:S(2)}) async-start(), calls=%async_computation.3 | async-start | bytes 3379200 | tf_op jit(solution)/shard_map/all_gather | solution.py:25
  8.2 189.0 %all-gather.3.cloned.1.call-start = ((), (), s32[]{:S(2)}) async-start(), calls=%async_computation.2 | async-start | bytes 10137600 | tf_op jit(solution)/shard_map/all_gather | solution.py:25
  16.9 8.7 %copy-start.3 = (f32[1280]{0:T(1024)S(1)}, f32[1280]{0:T(1024)}, u32[]{:S(2)}) copy-start(f32[1280]{0:T(1024)} %param.15) | copy-start | bytes 15364
  16.9 9.3 %copy-start.2 = (f32[3840]{0:T(1024)S(1)}, f32[3840]{0:T(1024)}, u32[]{:S(2)}) copy-start(f32[3840]{0:T(1024)} %param.17) | copy-start | bytes 46084
  16.9 9.9 %copy-start.4 = (f32[1280]{0:T(1024)S(1)}, f32[1280]{0:T(1024)}, u32[]{:S(2)}) copy-start(f32[1280]{0:T(1024)} %param.19) | copy-start | bytes 15364
  16.9 10.5 %copy-start.5 = (f32[1280]{0:T(1024)S(1)}, f32[1280]{0:T(1024)}, u32[]{:S(2)}) copy-start(f32[1280]{0:T(1024)} %param.20) | copy-start | bytes 15364
  16.9 11.7 %copy-start.1 = (s32[1,8,24]{2,1,0:T(8,128)S(1)}, s32[1,8,24]{2,1,0:T(8,128)}, u32[]{:S(2)}) copy-start(s32[1,8,24]{2,1,0:T(8,128)} %param.14) | copy-start | bytes 2308
  16.9 13.7 %copy-start.6 = (s32[1,128,1]{1,2,0:T(1,128)S(1)}, s32[1,128,1]{1,2,0:T(1,128)}, u32[]{:S(2)}) copy-start(s32[1,128,1]{1,2,0:T(1,128)} %param.21) | copy-start | bytes 1540
  16.9 113.8 %all-to-all-start = ((bf16[8,192,1280]{2,1,0:T(8,128)(2,1)}), bf16[8,192,1280]{2,1,0:T(8,128)(2,1)}, u32[]{:S(2)}, u32[]{:S(2)}) async-start(bf16[8,192,1280]{2,1,0:T(8,128)(2,1)} %bitcast.53), calls=%async_computation | async-start | bytes 7864320 | tf_op jit(solution)/shard_map/all_to_all | solution.py:194
Sparse Core Ops, SparseCore 0:
  10.2 100.0 all-gather.4
  113.3 83.8 all-gather.2

commit v2 on v1

--- a/solution.py
+++ b/solution.py
@@ -111,7 +111,7 @@
             ).astype(jnp.bfloat16)
 
 
-def encode(x, row_live, key_live, pick, norm_gain, qkv_w, qkv_bias, proj_w, proj_bias, merge_gain):
+def encode(x, row_live, key_live, pick, norm_gain, weights, qkv_bias, proj_bias, merge_gain):
     rows = x.shape[0]
     steps = 3 * D // CHUNK
     slots = pick.shape[0]
@@ -127,7 +127,7 @@
             full(1, D),
             pl.BlockSpec((D, CHUNK), lambda i: (0, i)),
             pl.BlockSpec((1, CHUNK), lambda i: (0, i)),
-            full(D, D),
+            pl.BlockSpec((D, D), lambda i: (0, 3)),
             full(1, D),
             full(1, D),
             full(rows, 1),
@@ -151,7 +151,7 @@
             flops=2 * rows * D * 4 * D, bytes_accessed=8 * D * D + 6 * rows * D, transcendentals=0
         ),
     )(
-        x, norm_gain[None], qkv_w, qkv_bias[None], proj_w, proj_bias[None], merge_gain[None],
+        x, norm_gain[None], weights, qkv_bias[None], weights, proj_bias[None], merge_gain[None],
         row_live, key_live, pick,
     )
 
@@ -210,9 +210,8 @@
         living.reshape(DST_WIN * WIN // PAIR, 1, PAIR),
         pick,
         norm_gain,
-        whole_weight(qkv_weight),
+        whole_weight(jnp.concatenate([qkv_weight, proj_weight], axis=1)),
         qkv_bias,
-        whole_weight(proj_weight),
         proj_bias,
         merge_gain,
     )

time: 279 us -> 259 us (0.928)
  waiting for transfers between devices: 157 us -> 138 us
    all_gather x2 -> x1, waiting for transfers between devices: 141 us -> 2.76 us  [whole_weight(): gathered = lax.all_gather(portion, ('section', 'dev'), axis=0, tiled=True)]
    all_to_all x1, waiting for transfers between devices: 16.5 us -> 136 us  [body(): lax.all_to_all(outgoing, 'dev', split_axis=0, concat_axis=0, tiled=True)]
    reshape x2 -> x1, local copies, waits for them, and re-layouts: 12.2 us -> 11.8 us  [whole_weight(): gathered.reshape(section_count, dev_count, sub_rows, shard.shape[1])]
  transfers between devices with their start and end apart: 3 -> 2, of which waited for: 3 -> 2; matrix products, arithmetic and copies ran while one was open for 9% -> 8% of each run, Pallas kernels for 0% -> 0%
where the time goes in v2:
time: 259 us
  waiting for transfers between devices  138 us (53%)
  blocking collectives  35.3 us (14%)
  Pallas kernels  29.2 us (11%)
  local copies, waits for them, and re-layouts  28.4 us (11%)
  between operations  13.5 us (5%)
  other arithmetic  7.17 us (3%)
  starting transfers between devices  6.5 us (3%)
    all_to_all x1, waiting for transfers between devices, body(): lax.all_to_all(outgoing, 'dev', split_axis=0, concat_axis=0, tiled=True)  136 us
    all_to_all x1, blocking collectives, body(): lax.all_to_all(packed, 'section', split_axis=0, concat_axis=0, tiled=True)  35.3 us
    pallas_call x1, Pallas kernels, encode(): pl.pallas_call(functools.partial(encode_kernel, steps), grid=(steps,), in...  29.2 us
    reshape x1, local copies, waits for them, and re-layouts, whole_weight(): gathered.reshape(section_count, dev_count, sub_rows, shard.shape[1])  11.8 us
    all_to_all x1, starting transfers between devices, body(): lax.all_to_all(outgoing, 'dev', split_axis=0, concat_axis=0, tiled=True)  6.5 us
  transfers between devices with their start and end apart: 2, of which 2 were waited for; matrix products, arithmetic and copies ran while one was open for 8% of the time, Pallas kernels for 0%

profile of v2, /device:TPU:0, one launch (start us, length us, event | category | flops | bytes accessed | tf_op | source)
XLA Modules:
  0.0 258.6 jit_solution(18033838993633816116)
XLA Ops:
  6.5 0.0 copy-start
  6.5 0.0 all-gather.2.cloned.1.call-start
  6.5 1.8 fusion
  8.3 0.0 all-gather.2.cloned.1.call-update
  8.3 0.8 select_reduce_fusion.1
  9.1 0.6 dynamic_slice.9
  9.7 0.7 select_reduce_fusion.2
  10.5 0.6 and_select_fusion.1
  11.1 0.1 compare_select_fusion
  11.2 0.1 reshape.312
  11.3 4.9 %gather_fusion = bf16[24,64,1280]{2,1,0:T(8,128)(2,1)} fusion(bf16[24,64,1280]{2,1,0:T(8,128)(2,1)} %bitcast.56, s32[1024]{0:T(1024)S(1)} %pad_clamp_fusion.2), kind=kCustom, calls=%fused_computation | custom fusion | bytes 7864416 | tf_op jit(solution)/shard_map/gather | solution.py:193
  16.2 0.0 copy-start.2
  16.2 0.0 copy-start.5
  16.2 6.5 %all-to-all-start = ((bf16[8,192,1280]{2,1,0:T(8,128)(2,1)}), bf16[8,192,1280]{2,1,0:T(8,128)(2,1)}, u32[]{:S(2)}, u32[]{:S(2)}) async-start(bf16[8,192,1280]{2,1,0:T(8,128)(2,1)} %bitcast.51), calls=%async_computation | async-start | bytes 7864320 | tf_op jit(solution)/shard_map/all_to_all | solution.py:194
  22.7 0.6 dynamic_slice.10
  23.3 0.1 lt.106
  23.4 0.6 multiply_add_fusion.1
  24.0 0.2 convert_reduce_fusion
  24.2 0.6 gather_fusion.1
  24.8 0.6 fusion.10
  25.5 0.0 copy-done
  25.5 0.6 gather_fusion.3
  26.1 0.1 mul.84
  26.2 0.1 lt.108
  26.3 0.1 lt.109
  26.4 0.0 copy-done.2
  26.4 0.6 broadcast_in_dim.22.gain_ref
  27.0 0.0 copy-done.3
  27.0 0.6 broadcast_in_dim.24.pb_ref
  27.6 0.0 copy-done.4
  27.6 0.6 broadcast_in_dim.25.mg_ref
  28.2 0.0 copy-done.1
  28.2 0.6 broadcast_in_dim.23.wb_ref
  28.8 0.0 copy-done.5
  28.8 0.1 fusion.2
  28.9 0.2 reduce_window_sum.11
  29.0 0.1 fusion.3
  29.1 0.9 reshape.342.row_ref
  30.0 0.2 select_reduce_fusion
  30.2 0.6 compare_convert_fusion.key_ref
  30.8 0.6 fusion.1.pick_ref
  31.4 135.7 %all-to-all-done = bf16[8,192,1280]{2,1,0:T(8,128)(2,1)} async-done(((bf16[8,192,1280]{2,1,0:T(8,128)(2,1)}), bf16[8,192,1280]{2,1,0:T(8,128)(2,1)}, u32[]{:S(2)}, u32[]{:S(2)}) %all-to-all-start) | async-done | bytes 3932192 | tf_op jit(solution)/shard_map/all_to_all | solution.py:194
  167.1 4.0 %gather_fusion.2 = bf16[8,64,1280]{2,1,0:T(8,128)(2,1)} fusion(bf16[24,64,1280]{2,1,0:T(8,128)(2,1)} %bitcast.5, s32[1024]{0:T(1024)S(1)} %pad_clamp_fusion), kind=kCustom, calls=%fused_computation.2 | custom fusion | bytes 2621472 | tf_op jit(solution)/shard_map/gather | solution.py:200
  171.1 2.8 %all-gather.2.cloned.1.call-done = bf16[1280,5120]{1,0:T(8,128)(2,1)} async-done(((bf16[40,5120]{1,0:T(8,128)(2,1)}), bf16[1280,5120]{1,0:T(8,128)(2,1)}) %all-gather.2.cloned.1.call-update) | async-done | bytes 13107216 | tf_op jit(solution)/shard_map/all_gather | solution.py:25
  173.9 11.8 %copy.15 = bf16[4,8,40,5120]{3,2,0,1:T(8,128)(2,1)} copy(bf16[4,8,40,5120]{3,2,1,0:T(8,128)(2,1)} %bitcast.52) | data formatting | bytes 26214400 | tf_op jit(solution)/shard_map/reshape | solution.py:27
  185.7 29.2 %shard_map.109 = bf16[256,5120]{1,0:T(8,128)(2,1)} custom-call(bf16[512,1280]{1,0:T(8,128)(2,1)} %bitcast.55, f32[1,1280]{1,0:T(1,128)} %broadcast_in_dim.22.gain_ref, bf16[1280,5120]{1,0:T(8,128)(2,1)} %bitcast.49, f32[1,3840]{1,0:T(1,128)} %broadcast_in_dim.23.wb_ref, bf16[1280,5120]{1,0:T(8,128)(2,1)} %bitcast.50, f32[1,1280]{1,0:T(1,128)} %broadcast_in_dim.24.pb_ref, ...), custom_call_target="tpu_custom_call" | custom-call | flops 6710886400 | bytes 17039360 | tf_op jit(solution)/shard_map/pallas_call | solution.py:122
  214.9 35.3 %all_to_all.18 = bf16[4,64,5120]{2,1,0:T(8,128)(2,1)S(1)} all-to-all(bf16[4,64,5120]{2,1,0:T(8,128)(2,1)} %bitcast.53), channel_id=1, replica_groups=mesh['section'=4,'dev'=8] {'section'}, dimensions={0} | all-to-all | bytes 5242880 | tf_op jit(solution)/shard_map/all_to_all | solution.py:218
  250.2 1.5 copy.18
  (11 shorter events, 0.1 us)
Async XLA Ops:
  6.5 18.9 %copy-start = (s32[1,8,24]{2,1,0:T(8,128)S(1)}, s32[1,8,24]{2,1,0:T(8,128)}, u32[]{:S(2)}) copy-start(s32[1,8,24]{2,1,0:T(8,128)} %param.14) | copy-start | bytes 2308
  6.5 167.4 %all-gather.2.cloned.1.call-start = ((), (), s32[]{:S(2)}) async-start(), calls=%async_computation.2 | async-start | bytes 13516800 | tf_op jit(solution)/shard_map/all_gather | solution.py:25
  16.2 10.2 %copy-start.2 = (f32[1280]{0:T(1024)S(1)}, f32[1280]{0:T(1024)}, u32[]{:S(2)}) copy-start(f32[1280]{0:T(1024)} %param.15) | copy-start | bytes 15364
  16.2 10.8 %copy-start.3 = (f32[1280]{0:T(1024)S(1)}, f32[1280]{0:T(1024)}, u32[]{:S(2)}) copy-start(f32[1280]{0:T(1024)} %param.19) | copy-start | bytes 15364
  16.2 11.4 %copy-start.4 = (f32[1280]{0:T(1024)S(1)}, f32[1280]{0:T(1024)}, u32[]{:S(2)}) copy-start(f32[1280]{0:T(1024)} %param.20) | copy-start | bytes 15364
  16.2 12.0 %copy-start.1 = (f32[3840]{0:T(1024)S(1)}, f32[3840]{0:T(1024)}, u32[]{:S(2)}) copy-start(f32[3840]{0:T(1024)} %param.17) | copy-start | bytes 46084
  16.2 12.6 %copy-start.5 = (s32[1,128,1]{1,2,0:T(1,128)S(1)}, s32[1,128,1]{1,2,0:T(1,128)}, u32[]{:S(2)}) copy-start(s32[1,128,1]{1,2,0:T(1,128)} %param.21) | copy-start | bytes 1540
  16.2 150.9 %all-to-all-start = ((bf16[8,192,1280]{2,1,0:T(8,128)(2,1)}), bf16[8,192,1280]{2,1,0:T(8,128)(2,1)}, u32[]{:S(2)}, u32[]{:S(2)}) async-start(bf16[8,192,1280]{2,1,0:T(8,128)(2,1)} %bitcast.51), calls=%async_computation | async-start | bytes 7864320 | tf_op jit(solution)/shard_map/all_to_all | solution.py:194
Sparse Core Ops, SparseCore 0:
  10.2 163.6 all-gather.1
